TPU v7x, 32 devices: a whole 2x2x4 slice. The times are simulated.
32 devices in a mesh: dp: 4 (over x, core), vocab: 8 (over z, y).
Axes of the slice: x: 2, y: 2, z: 4, core: 2. Of those that a mesh axis runs over, the one named last changes fastest.
Arguments:
- policy_hidden: bfloat16 [512, 4096], P('dp'), may hold values from -84 to 84
- policy_weight: bfloat16 [4096, 65536], P('dp', 'vocab'), may hold values from -0.09375 to 0.09375
- reference_hidden: bfloat16 [512, 4096], P(('dp', 'vocab')), may hold values from -84 to 84
- reference_weight: bfloat16 [4096, 65536], P(None, ('dp', 'vocab')), may hold values from -0.09375 to 0.09375
- targets: int32 [512], replicated, may hold values from 0 to 65535
- response_mask: int32 [512], replicated, may hold values 0 or 1
- pair_index: int32 [16], replicated, may hold values from 0 to 15, each once
Outputs:
- hidden_grad: bfloat16 [512, 4096], P('vocab', 'dp')
- weight_grad: bfloat16 [4096, 65536], P('dp', 'vocab')
- total_loss: float32 [], replicated
Inputs may be any that keep to these rules, and one draw needn't show every extreme that they name: `pair_index`: each number of 0 to 15 once; entries 2p and 2p + 1 are the chosen and the rejected sequence of pair p.
All inputs are finite; a program needn't handle non-finite values.
Results may differ from a plain program's by a relative error of at most 0.005.
The roundings to bfloat16 on the way count: a program that leaves them out, or rounds other values in their place, can miss the bound.
Values may be sent and summed in bfloat16 or wider, within the bound.
A program may use at most 128 MiB of HBM per device.

v0:
```python
import jax
import jax.numpy as jnp
from jax import lax
from jax.sharding import PartitionSpec as P

SEQ_LEN = 32
beta = 0.1
loss_scale = 4096.0


def pair_terms(log_ratio, pair_index):
    chosen = pair_index[0::2]
    rejected = pair_index[1::2]
    margin = beta * (log_ratio[chosen] - log_ratio[rejected])
    pair_count = chosen.shape[0]
    total_loss = jnp.sum(jax.nn.softplus(-margin)) / pair_count
    weight = -beta * loss_scale * jax.nn.sigmoid(-margin) / pair_count
    numbers = jnp.arange(log_ratio.shape[0], dtype=jnp.int32)[:, None]
    factor = jnp.sum(
        jnp.where(numbers == chosen[None, :], weight[None, :], 0.0)
        - jnp.where(numbers == rejected[None, :], weight[None, :], 0.0),
        axis=1,
    )
    return (total_loss, factor)


def local_pick(logits, targets, offset, axis):
    column_ids = lax.broadcasted_iota(jnp.int32, logits.shape, axis)
    shifted = targets - offset
    wanted = shifted[:, None]
    return jnp.sum(jnp.where(column_ids == wanted, logits, 0.0), axis=axis)


def local(
    policy_hidden,
    policy_weight,
    reference_hidden,
    reference_weight,
    targets,
    response_mask,
    pair_index,
):
    data_index = lax.axis_index("dp")
    vocab_index = lax.axis_index("vocab")
    vocab_devices = lax.axis_size("vocab")
    local_tokens = policy_hidden.shape[0]
    policy_width = policy_weight.shape[1]
    reference_width = reference_weight.shape[1]
    active = response_mask.astype(jnp.float32)
    columns = lax.all_to_all(policy_hidden, "dp", split_axis=1, concat_axis=0, tiled=True)
    reference_logits = jnp.dot(
        lax.all_gather(reference_hidden, ("dp", "vocab"), axis=0, tiled=True),
        reference_weight,
        preferred_element_type=jnp.float32,
    )
    reference_offset = (data_index * vocab_devices + vocab_index) * reference_width
    reference_top = jnp.max(reference_logits, axis=1)
    reference_pick = local_pick(reference_logits, targets, reference_offset, 1)
    policy_logits = lax.psum_scatter(
        jnp.dot(columns, policy_weight, preferred_element_type=jnp.float32),
        "dp",
        scatter_dimension=0,
        tiled=True,
    )
    own_targets = lax.dynamic_slice_in_dim(targets, data_index * local_tokens, local_tokens, 0)
    policy_offset = vocab_index * policy_width
    policy_pick = local_pick(policy_logits, own_targets, policy_offset, 1)
    policy_max = lax.pmax(jnp.max(policy_logits, axis=1), "vocab")
    policy_sum, policy_picked = lax.psum(
        (jnp.sum(jnp.exp(policy_logits - policy_max[:, None]), axis=1), policy_pick), "vocab"
    )
    policy_total = policy_max + jnp.log(policy_sum)
    reference_max = lax.pmax(reference_top, ("dp", "vocab"))
    reference_sum, reference_picked = lax.psum(
        (jnp.sum(jnp.exp(reference_logits - reference_max[:, None]), axis=1), reference_pick),
        ("dp", "vocab"),
    )
    reference_logp = reference_picked - reference_max - jnp.log(reference_sum)
    own_reference = lax.dynamic_slice_in_dim(
        reference_logp, data_index * local_tokens, local_tokens, 0
    )
    own_active = lax.dynamic_slice_in_dim(active, data_index * local_tokens, local_tokens, 0)
    own_ratio = jnp.sum(
        (own_active * (policy_picked - policy_total - own_reference)).reshape(-1, SEQ_LEN), axis=1
    )
    log_ratio = lax.all_gather(own_ratio, "dp", axis=0, tiled=True)
    total_loss, factor = pair_terms(log_ratio, pair_index)
    token_scale = lax.dynamic_slice_in_dim(
        active * jnp.repeat(factor, SEQ_LEN), data_index * local_tokens, local_tokens, 0
    )
    column_ids = lax.broadcasted_iota(jnp.int32, policy_logits.shape, 1)
    onehot = (column_ids == (own_targets - policy_offset)[:, None]).astype(jnp.float32)
    logit_grad = (
        token_scale[:, None] * (onehot - jnp.exp(policy_logits - policy_total[:, None]))
    ).astype(jnp.bfloat16)
    segment = lax.all_gather(logit_grad, "dp", axis=0, tiled=True)
    weight_grad = lax.dot_general(
        columns, segment, (((0,), (0,)), ((), ())), preferred_element_type=jnp.float32
    )
    hidden_piece = lax.dot_general(
        segment, policy_weight, (((1,), (1,)), ((), ())), preferred_element_type=jnp.float32
    )
    weight_grad, hidden_part = (weight_grad, hidden_piece)
    hidden_grad = lax.psum_scatter(hidden_part, "vocab", scatter_dimension=0, tiled=True)
    return (hidden_grad.astype(jnp.bfloat16), weight_grad.astype(jnp.bfloat16), total_loss)


def solution(mesh):
    placed = (
        P("dp", None),
        P("dp", "vocab"),
        P(("dp", "vocab"), None),
        P(None, ("dp", "vocab")),
        P(),
        P(),
        P(),
    )
    return jax.shard_map(
        local,
        mesh=mesh,
        in_specs=placed,
        out_specs=(P("vocab", "dp"), P("dp", "vocab"), P()),
        check_vma=False,
    )
```

profile of v0, /device:TPU:0, one launch (start us, length us, event | category | flops | bytes accessed | tf_op | source)
XLA Modules:
  0.0 385.9 jit_solution(17941225385931187928)
XLA Ops:
  8.0 0.0 all-gather.3.cloned.1.call-start
  8.0 0.7 all-gather.3.cloned.1.call-update
  8.7 0.0 reduce-scatter.3.cloned.1.call-start
  8.8 1.6 copy.15
  10.4 19.4 %all_to_all.19 = bf16[128,4,1024]{0,2,1:T(8,128)(2,1)S(1)} all-to-all(bf16[128,4,1024]{0,2,1:T(8,128)(2,1)S(1)} %bitcast.15), channel_id=1, replica_groups=mesh['dp'=4,'vocab'=8] {'dp'}, dimensions={1} | all-to-all | bytes 2097152 | tf_op jit(solution)/shard_map/all_to_all | solution.py:50
  29.8 0.5 copy.16
  30.4 15.8 %fusion.2 = f32[512,8192]{1,0:T(8,128)} fusion(bf16[512,1024]{1,0:T(8,128)(2,1)S(1)} %bitcast.16, bf16[1024,8192]{1,0:T(8,128)(2,1)} %param.8), kind=kOutput, calls=%fused_computation.28 | convolution fusion | flops 8589934592 | bytes 34603008 | tf_op jit(solution)/shard_map/dot_general | solution.py:60
  46.2 0.0 reduce-scatter.3.cloned.1.call-update
  46.2 0.0 all-gather.5.cloned.1.call-start
  46.3 0.6 copy-done.2
  46.8 0.1 slice.7
  46.9 0.1 slice.6
  47.0 0.0 copy-done
  47.1 0.6 dynamic-slice
  48.3 0.0 copy-done.1
  48.3 0.1 dynamic-slice_subtract_fusion
  48.4 28.4 %all-gather.3.cloned.1.call-done = bf16[512,4096]{1,0:T(8,128)(2,1)} async-done(((bf16[16,4096]{1,0:T(8,128)(2,1)}), bf16[512,4096]{1,0:T(8,128)(2,1)}) %all-gather.3.cloned.1.call-update) | async-done | bytes 4194320 | tf_op jit(solution)/shard_map/all_gather | solution.py:52
  76.8 15.7 %fusion.1 = (f32[512]{0:T(512)S(1)}, f32[512,2048]{1,0:T(8,128)}) fusion(bf16[512,4096]{1,0:T(8,128)(2,1)} %all-gather.3.cloned.1.call-done, bf16[4096,2048]{1,0:T(8,128)(2,1)} %param.10), kind=kOutput, calls=%fused_computation.27 | convolution fusion | flops 8590983168 | bytes 25167872 | tf_op jit(solution)/shard_map/dot_general | solution.py:51
  92.5 40.3 %pmax.15 = f32[512]{0:T(512)S(1)} all-reduce(f32[512]{0:T(512)S(1)} %get-tuple-element.27), channel_id=1, replica_groups=mesh['dp'=4,'vocab'=8] {'dp','vocab'}, use_global_device_ids=true, to_apply=%region_10.11 | all-reduce | flops 512 | bytes 4096 | tf_op jit(solution)/shard_map/pmax | solution.py:73
  132.8 3.6 select_reduce_fusion
  136.5 41.4 %all-reduce.1 = (f32[512]{0:T(512)S(1)}, f32[512]{0:T(512)S(1)}) all-reduce(f32[512]{0:T(512)S(1)} %get-tuple-element.18, f32[512]{0:T(512)S(1)} %get-tuple-element.17), channel_id=1, replica_groups=mesh['dp'=4,'vocab'=8] {'dp','vocab'}, use_global_device_ids=true, to_apply=%region_12.13 | all-reduce | flops 1024 | bytes 8192 | tf_op jit(solution)/shard_map/psum | solution.py:74
  177.9 0.0 reduce-scatter.3.cloned.1.call-done
  177.9 2.5 reduce_max.18
  180.3 20.9 %pmax.14 = f32[128]{0:T(128)S(1)} all-reduce(f32[128]{0:T(128)S(1)} %reduce_max.18), channel_id=1, replica_groups=mesh['dp'=4,'vocab'=8] {'vocab'}, use_global_device_ids=true, to_apply=%region_4.5 | all-reduce | flops 128 | bytes 1024 | tf_op jit(solution)/shard_map/pmax | solution.py:68
  201.2 3.4 select_reduce_fusion.1
  204.6 17.1 %all-reduce.2 = (f32[128]{0:T(128)S(1)}, f32[128]{0:T(128)S(1)}) all-reduce(f32[128]{0:T(128)S(1)} %get-tuple-element.16, f32[128]{0:T(128)S(1)} %get-tuple-element.15), channel_id=1, replica_groups=mesh['dp'=4,'vocab'=8] {'vocab'}, use_global_device_ids=true, to_apply=%region_6.7 | all-reduce | flops 256 | bytes 2048 | tf_op jit(solution)/shard_map/psum | solution.py:69
  221.8 0.1 subtract_multiply_fusion.1
  221.8 0.1 reshape.33
  221.9 0.1 reduce_sum.67
  222.1 0.2 dynamic-update-slice
  222.3 5.6 %all-reduce = f32[16]{0:T(128)S(1)} all-reduce(f32[16]{0:T(128)S(1)} %dynamic-update-slice), channel_id=1, replica_groups=mesh['dp'=4,'vocab'=8] {'dp'}, use_global_device_ids=true, to_apply=%add | all-reduce | flops 16 | bytes 128
  227.9 0.6 gather_fusion
  228.6 0.6 gather_fusion.1
  229.2 0.6 fusion
  229.8 0.1 subtract_reduce_fusion
  229.9 0.1 broadcast_in_dim.51
  230.0 0.1 reshape.34
  230.1 0.1 dynamic_slice.15
  230.2 4.7 %multiply_convert_fusion = bf16[128,8192]{1,0:T(8,128)(2,1)} fusion(f32[128,8192]{1,0:T(8,128)} %reduce-scatter.3.cloned.1.call-done, f32[128]{0:T(128)S(1)} %get-tuple-element.24, f32[128]{0:T(128)S(1)} %dynamic_slice.15, s32[128]{0:T(128)S(1)} %dynamic-slice_subtract_fusion), kind=kLoop, calls=%fused_computation.3 | loop fusion | flops 6291456 | bytes 6292992 | tf_op jit(solution)/shard_map/convert_element_type | solution.py:95
  234.9 0.0 all-gather.5.cloned.1.call-update
  234.9 0.0 reduce-scatter.5.cloned.1.call-start
  235.0 56.3 %all-gather.5.cloned.1.call-done = bf16[512,8192]{1,0:T(8,128)(2,1)} async-done(((bf16[128,8192]{1,0:T(8,128)(2,1)}), bf16[512,8192]{1,0:T(8,128)(2,1)}) %all-gather.5.cloned.1.call-update) | async-done | bytes 8388624 | tf_op jit(solution)/shard_map/all_gather | solution.py:96
  291.2 15.9 %fusion.3 = f32[512,1024]{1,0:T(8,128)} fusion(bf16[512,8192]{1,0:T(8,128)(2,1)} %all-gather.5.cloned.1.call-done, bf16[1024,8192]{1,0:T(8,128)(2,1)} %param.8), kind=kOutput, calls=%fused_computation.29 | convolution fusion | flops 8589934592 | bytes 27262976 | tf_op jit(solution)/shard_map/dot_general | solution.py:100
  307.1 0.0 reduce-scatter.5.cloned.1.call-update
  307.8 15.9 %convert_bitcast_fusion = bf16[1024,8192]{0,1:T(8,128)(2,1)} fusion(bf16[512,8192]{1,0:T(8,128)(2,1)} %all-gather.5.cloned.1.call-done, bf16[512,1024]{1,0:T(8,128)(2,1)S(1)} %bitcast.17), kind=kOutput, calls=%fused_computation.2 | convolution fusion | flops 8598323200 | bytes 26214400 | tf_op jit(solution)/shard_map/dot_general | solution.py:97
  323.7 21.3 %copy.17 = bf16[1024,8192]{1,0:T(8,128)(2,1)} copy(bf16[1024,8192]{0,1:T(8,128)(2,1)} %convert_bitcast_fusion) | data formatting | bytes 33554432
  345.0 30.7 %reduce-scatter.5.cloned.1.call-done = f32[64,1024]{1,0:T(8,128)} async-done(((f32[512,1024]{1,0:T(8,128)}), f32[64,1024]{1,0:T(8,128)}) %reduce-scatter.5.cloned.1.call-update) | async-done | bytes 262160 | tf_op jit(solution)/shard_map/reduce_scatter | solution.py:104
  375.8 1.6 convert_element_type.21
  (14 shorter events, 0.1 us)
Async XLA Ops:
  8.0 68.8 %all-gather.3.cloned.1.call-start = ((), (), s32[]{:S(2)}) async-start(), calls=%async_computation.4 | async-start | bytes 4325376 | tf_op jit(solution)/shard_map/all_gather | solution.py:52
  8.7 169.1 %reduce-scatter.3.cloned.1.call-start = ((), (), s32[]{:S(2)}) async-start(), calls=%async_computation.3 | async-start | bytes 20971520 | tf_op jit(solution)/shard_map/reduce_scatter | solution.py:59
  46.2 0.7 copy-start.2
  46.2 0.8 copy-start
  46.2 0.9 copy-start.3
  46.2 2.1 copy-start.1
  46.2 245.0 %all-gather.5.cloned.1.call-start = ((), (), s32[]{:S(2)}) async-start(), calls=%async_computation.5 | async-start | bytes 10485760 | tf_op jit(solution)/shard_map/all_gather | solution.py:96
  234.9 140.8 %reduce-scatter.5.cloned.1.call-start = ((), (), s32[]{:S(2)}) async-start(), calls=%async_computation.6 | async-start | bytes 2359296 | tf_op jit(solution)/shard_map/reduce_scatter | solution.py:104
Sparse Core Ops, SparseCore 0:
  11.9 64.9 all-gather.2
  307.3 68.4 reduce-scatter.4
Sparse Core Ops, SparseCore 1:
  46.3 128.4 reduce-scatter.2
  235.0 56.2 all-gather.4
where the time goes:
time: 387 us; the launch traced here: 386 us
  blocking collectives  145 us (37%)
  waiting for transfers between devices  116 us (30%)
  matrix products  63.3 us (16%)
  local copies, waits for them, and re-layouts  26.6 us (7%)
  between operations  18 us (5%)
  other arithmetic  16.9 us (4%)
    all_gather x1, waiting for transfers between devices, local(): segment = lax.all_gather(logit_grad, 'dp', axis=0, tiled=True)  56.3 us
    psum x1, blocking collectives, local(): lax.psum((jnp.sum(jnp.exp(reference_logits - reference_max[:, None]), axi...  41.4 us
    pmax x1, blocking collectives, local(): reference_max = lax.pmax(reference_top, ('dp', 'vocab'))  40.3 us
    reduce_scatter x1, waiting for transfers between devices, local(): lax.psum_scatter(hidden_part, 'vocab', scatter_dimension=0, tiled=True)  30.7 us
    all_gather x1, waiting for transfers between devices, local(): lax.all_gather(reference_hidden, ('dp', 'vocab'), axis=0, tiled=True)  28.4 us
    unnamed x13, local copies, waits for them, and re-layouts  24.3 us
    pmax x1, blocking collectives, local(): policy_max = lax.pmax(jnp.max(policy_logits, axis=1), 'vocab')  20.9 us
    all_to_all x1, blocking collectives, local(): lax.all_to_all(policy_hidden, 'dp', split_axis=1, concat_axis=0, tiled=True)  19.4 us
  transfers between devices with their start and end apart: 4, of which 3 were waited for; matrix products, arithmetic and copies ran while one was open for 20% of the time, Pallas kernels for 0%

commit v1 on v0

--- a/solution.py
+++ b/solution.py
@@ -2,6 +2,7 @@
 import jax.numpy as jnp
 from jax import lax
 from jax.sharding import PartitionSpec as P
+from jax.lax import axis_index, ppermute, psum
 
 SEQ_LEN = 32
 beta = 0.1
@@ -93,7 +94,27 @@
     logit_grad = (
         token_scale[:, None] * (onehot - jnp.exp(policy_logits - policy_total[:, None]))
     ).astype(jnp.bfloat16)
-    segment = lax.all_gather(logit_grad, "dp", axis=0, tiled=True)
+    val2 = psum(1, "dp")
+    u_next = axis_index("dp")
+    left_arr, before, p_next = (val2, u_next, logit_grad.shape[0])
+    rack = [(dev, (dev + 1) % left_arr) for dev in range(left_arr)]
+    sheets = [(dev, (dev - 1) % left_arr) for dev in range(left_arr)]
+    segment = jnp.zeros(
+        (*logit_grad.shape[:0], left_arr * p_next, *logit_grad.shape[1:]), logit_grad.dtype
+    )
+    segment = lax.dynamic_update_slice_in_dim(segment, logit_grad, before * p_next, axis=0)
+    piece_now = response = logit_grad
+    formed = left_arr // 2
+    for ii in range(1, formed + 1):
+        piece_now = ppermute(piece_now, axis_name="dp", perm=rack)
+        segment = lax.dynamic_update_slice_in_dim(
+            segment, piece_now, (before - ii) % left_arr * p_next, axis=0
+        )
+        if ii < left_arr - formed:
+            response = ppermute(response, "dp", sheets)
+            segment = lax.dynamic_update_slice_in_dim(
+                segment, response, (before + ii) % left_arr * p_next, axis=0
+            )
     weight_grad = lax.dot_general(
         columns, segment, (((0,), (0,)), ((), ())), preferred_element_type=jnp.float32
     )

time: 387 us -> 407 us (1.052)
  local copies, waits for them, and re-layouts: 26.6 us -> 41.5 us
  waiting for transfers between devices: 116 us -> 122 us
    ppermute x0 -> x3, waiting for transfers between devices: none -> 64.8 us  [the longest x2 64.8 us: local(): piece_now = ppermute(piece_now, axis_name='dp', perm=rack)]
    all_gather x1 -> x0, waiting for transfers between devices: 56.3 us -> none  [local(): segment = lax.all_gather(logit_grad, 'dp', axis=0, tiled=True)]
    dynamic_update_slice x0 -> x3, local copies, waits for them, and re-layouts: none -> 9.29 us  [the longest x2 6.19 us: local(): lax.dynamic_update_slice_in_dim(segment, piece_now, (before - ii) % left_...]
    convert_element_type x1 -> x0, other arithmetic: 4.73 us -> none  [local(): logit_grad = (token_scale[:, None] * (onehot - jnp.exp(policy_logits - po...]
    unnamed x13 -> x17, local copies, waits for them, and re-layouts: 24.3 us -> 28.9 us
  transfers between devices with their start and end apart: 4 -> 6, of which waited for: 3 -> 4; matrix products, arithmetic and copies ran while one was open for 20% -> 20% of each run, Pallas kernels for 0% -> 0%
where the time goes in v1:
time: 407 us; the launch traced here: 405 us
  blocking collectives  145 us (36%)
  waiting for transfers between devices  122 us (30%)
  matrix products  63.3 us (16%)
  local copies, waits for them, and re-layouts  41.5 us (10%)
  between operations  18 us (4%)
  other arithmetic  13.6 us (3%)
    ppermute x2, waiting for transfers between devices, local(): piece_now = ppermute(piece_now, axis_name='dp', perm=rack)  64.8 us
    psum x1, blocking collectives, local(): lax.psum((jnp.sum(jnp.exp(reference_logits - reference_max[:, None]), axi...  41.4 us
    pmax x1, blocking collectives, local(): reference_max = lax.pmax(reference_top, ('dp', 'vocab'))  40.3 us
    unnamed x17, local copies, waits for them, and re-layouts  28.9 us
    reduce_scatter x1, waiting for transfers between devices, local(): lax.psum_scatter(hidden_part, 'vocab', scatter_dimension=0, tiled=True)  28.5 us
    all_gather x1, waiting for transfers between devices, local(): lax.all_gather(reference_hidden, ('dp', 'vocab'), axis=0, tiled=True)  28.4 us
    pmax x1, blocking collectives, local(): policy_max = lax.pmax(jnp.max(policy_logits, axis=1), 'vocab')  20.8 us
    all_to_all x1, blocking collectives, local(): lax.all_to_all(policy_hidden, 'dp', split_axis=1, concat_axis=0, tiled=True)  19.4 us
  transfers between devices with their start and end apart: 6, of which 4 were waited for; matrix products, arithmetic and copies ran while one was open for 20% of the time, Pallas kernels for 0%

profile of v1, /device:TPU:0, one launch (start us, length us, event | category | flops | bytes accessed | tf_op | source)
XLA Modules:
  0.0 405.4 jit_solution(17034184875286300246)
XLA Ops:
  8.0 0.7 all-gather.2.cloned.1.call-update
  8.7 0.0 reduce-scatter.3.cloned.1.call-start
  8.8 1.6 copy.15
  10.4 19.4 %all_to_all.19 = bf16[128,4,1024]{0,2,1:T(8,128)(2,1)S(1)} all-to-all(bf16[128,4,1024]{0,2,1:T(8,128)(2,1)S(1)} %bitcast.15), channel_id=1, replica_groups=mesh['dp'=4,'vocab'=8] {'dp'}, dimensions={1} | all-to-all | bytes 2097152 | tf_op jit(solution)/shard_map/all_to_all | solution.py:51
  29.8 0.5 copy.16
  30.3 15.8 %fusion.2 = f32[512,8192]{1,0:T(8,128)} fusion(bf16[512,1024]{1,0:T(8,128)(2,1)S(1)} %bitcast.16, bf16[1024,8192]{1,0:T(8,128)(2,1)} %param.8), kind=kOutput, calls=%fused_computation.32 | convolution fusion | flops 8589934592 | bytes 34603008 | tf_op jit(solution)/shard_map/dot_general | solution.py:61
  46.2 0.0 reduce-scatter.5.cloned.1.call-start
  46.3 0.6 copy-done.4
  46.8 0.1 slice.7
  46.9 0.1 slice.6
  47.1 0.6 dynamic-slice
  48.3 0.1 dynamic-slice_subtract_fusion
  48.4 28.4 %all-gather.2.cloned.1.call-done = bf16[512,4096]{1,0:T(8,128)(2,1)} async-done(((bf16[16,4096]{1,0:T(8,128)(2,1)}), bf16[512,4096]{1,0:T(8,128)(2,1)}) %all-gather.2.cloned.1.call-update) | async-done | bytes 4194320 | tf_op jit(solution)/shard_map/all_gather | solution.py:53
  76.8 15.7 %fusion.1 = (f32[512]{0:T(512)S(1)}, f32[512,2048]{1,0:T(8,128)}) fusion(bf16[512,4096]{1,0:T(8,128)(2,1)} %all-gather.2.cloned.1.call-done, bf16[4096,2048]{1,0:T(8,128)(2,1)} %param.10), kind=kOutput, calls=%fused_computation.31 | convolution fusion | flops 8590983168 | bytes 25167872 | tf_op jit(solution)/shard_map/dot_general | solution.py:52
  92.5 40.3 %pmax.15 = f32[512]{0:T(512)S(1)} all-reduce(f32[512]{0:T(512)S(1)} %get-tuple-element.29), channel_id=1, replica_groups=mesh['dp'=4,'vocab'=8] {'dp','vocab'}, use_global_device_ids=true, to_apply=%region_10.11 | all-reduce | flops 512 | bytes 4096 | tf_op jit(solution)/shard_map/pmax | solution.py:74
  132.8 3.6 select_reduce_fusion
  136.5 41.4 %all-reduce.1 = (f32[512]{0:T(512)S(1)}, f32[512]{0:T(512)S(1)}) all-reduce(f32[512]{0:T(512)S(1)} %get-tuple-element.18, f32[512]{0:T(512)S(1)} %get-tuple-element.17), channel_id=1, replica_groups=mesh['dp'=4,'vocab'=8] {'dp','vocab'}, use_global_device_ids=true, to_apply=%region_12.13 | all-reduce | flops 1024 | bytes 8192 | tf_op jit(solution)/shard_map/psum | solution.py:75
  177.9 2.5 reduce_max.18
  180.3 20.8 %pmax.14 = f32[128]{0:T(128)S(1)} all-reduce(f32[128]{0:T(128)S(1)} %reduce_max.18), channel_id=1, replica_groups=mesh['dp'=4,'vocab'=8] {'vocab'}, use_global_device_ids=true, to_apply=%region_4.5 | all-reduce | flops 128 | bytes 1024 | tf_op jit(solution)/shard_map/pmax | solution.py:69
  201.2 3.4 select_reduce_fusion.1
  204.6 17.1 %all-reduce.2 = (f32[128]{0:T(128)S(1)}, f32[128]{0:T(128)S(1)}) all-reduce(f32[128]{0:T(128)S(1)} %get-tuple-element.16, f32[128]{0:T(128)S(1)} %get-tuple-element.15), channel_id=1, replica_groups=mesh['dp'=4,'vocab'=8] {'vocab'}, use_global_device_ids=true, to_apply=%region_6.7 | all-reduce | flops 256 | bytes 2048 | tf_op jit(solution)/shard_map/psum | solution.py:70
  221.8 0.1 subtract_multiply_fusion.1
  221.8 0.1 reshape.33
  221.9 0.1 reduce_sum.67
  222.0 0.2 dynamic-update-slice
  222.3 5.6 %all-reduce = f32[16]{0:T(128)S(1)} all-reduce(f32[16]{0:T(128)S(1)} %dynamic-update-slice), channel_id=1, replica_groups=mesh['dp'=4,'vocab'=8] {'dp'}, use_global_device_ids=true, to_apply=%add | all-reduce | flops 16 | bytes 128
  227.9 0.6 gather_fusion
  228.6 0.6 gather_fusion.1
  229.2 0.6 fusion
  229.8 0.1 subtract_reduce_fusion
  229.9 0.1 broadcast_in_dim.55
  230.0 0.1 reshape.34
  230.1 0.1 dynamic_slice.15
  230.2 1.0 broadcast_in_dim.48
  231.2 1.2 copy-done
  232.4 1.4 constant_dynamic-update-slice_fusion.3
  233.7 3.4 copy-done.1
  237.1 1.7 collective-permute-start.1
  238.9 45.3 %collective-permute-done = bf16[128,8192]{1,0:T(8,128)(2,1)} collective-permute-done((bf16[128,8192]{1,0:T(8,128)(2,1)S(1)}, bf16[128,8192]{1,0:T(8,128)(2,1)}, u32[]{:S(2)}, u32[]{:S(2)}) %collective-permute-start) | collective-permute-done | bytes 2097184 | tf_op jit(solution)/shard_map/ppermute | solution.py:109
  284.1 3.1 constant_dynamic-update-slice_fusion.2
  287.2 3.1 constant_dynamic-update-slice_fusion.1
  290.3 19.6 %collective-permute-done.2 = bf16[128,8192]{1,0:T(8,128)(2,1)} collective-permute-done((bf16[128,8192]{1,0:T(8,128)(2,1)}, bf16[128,8192]{1,0:T(8,128)(2,1)}, u32[]{:S(2)}, u32[]{:S(2)}) %collective-permute-start.2) | collective-permute-done | bytes 2097184 | tf_op jit(solution)/shard_map/ppermute | solution.py:109
  309.9 3.1 constant_dynamic-update-slice_fusion
  313.0 15.8 %fusion.3 = f32[512,1024]{1,0:T(8,128)} fusion(bf16[512,8192]{1,0:T(8,128)(2,1)} %constant_dynamic-update-slice_fusion, bf16[1024,8192]{1,0:T(8,128)(2,1)} %param.8), kind=kOutput, calls=%fused_computation.33 | convolution fusion | flops 8589934592 | bytes 27262976 | tf_op jit(solution)/shard_map/dot_general | solution.py:121
  329.5 15.9 %convert_bitcast_fusion = bf16[1024,8192]{0,1:T(8,128)(2,1)} fusion(bf16[512,8192]{1,0:T(8,128)(2,1)} %constant_dynamic-update-slice_fusion, bf16[512,1024]{1,0:T(8,128)(2,1)S(1)} %bitcast.17), kind=kOutput, calls=%fused_computation.2 | convolution fusion | flops 8598323200 | bytes 26214400 | tf_op jit(solution)/shard_map/dot_general | solution.py:118
  345.4 21.3 %copy.17 = bf16[1024,8192]{1,0:T(8,128)(2,1)} copy(bf16[1024,8192]{0,1:T(8,128)(2,1)} %convert_bitcast_fusion) | data formatting | bytes 33554432
  366.7 28.5 %reduce-scatter.5.cloned.1.call-done = f32[64,1024]{1,0:T(8,128)} async-done(((f32[512,1024]{1,0:T(8,128)}), f32[64,1024]{1,0:T(8,128)}) %reduce-scatter.5.cloned.1.call-update) | async-done | bytes 262160 | tf_op jit(solution)/shard_map/reduce_scatter | solution.py:125
  395.2 1.6 convert_element_type.21
  (24 shorter events, 0.2 us)
Async XLA Ops:
  8.0 68.8 %all-gather.2.cloned.1.call-start = ((), (), s32[]{:S(2)}) async-start(), calls=%async_computation.4 | async-start | bytes 4325376 | tf_op jit(solution)/shard_map/all_gather | solution.py:53
  8.7 169.1 %reduce-scatter.3.cloned.1.call-start = ((), (), s32[]{:S(2)}) async-start(), calls=%async_computation.3 | async-start | bytes 20971520 | tf_op jit(solution)/shard_map/reduce_scatter | solution.py:60
  46.2 0.7 copy-start.4
  46.2 0.8 copy-start.2
  46.2 0.9 copy-start.5
  46.2 2.1 copy-start.3
  46.2 349.0 %reduce-scatter.5.cloned.1.call-start = ((), (), s32[]{:S(2)}) async-start(), calls=%async_computation.5 | async-start | bytes 2359296 | tf_op jit(solution)/shard_map/reduce_scatter | solution.py:125
  230.2 2.2 copy-start
  233.7 3.4 copy-start.1
  237.1 47.0 %collective-permute-start = (bf16[128,8192]{1,0:T(8,128)(2,1)S(1)}, bf16[128,8192]{1,0:T(8,128)(2,1)}, u32[]{:S(2)}, u32[]{:S(2)}) collective-permute-start(bf16[128,8192]{1,0:T(8,128)(2,1)S(1)} %get-tuple-element.24), channel_id=1, source_target_pairs={{0,8},{8,16},{16,24},{24,0},{1,9},{9,17},{17,25},{25,1},{2,10},{10... | collective-permute-start | bytes 6291464 | tf_op jit(solution)/shard_map/ppermute | solution.py:109
  237.1 50.1 %collective-permute-start.1 = (bf16[128,8192]{1,0:T(8,128)(2,1)S(1)}, bf16[128,8192]{1,0:T(8,128)(2,1)}, u32[]{:S(2)}, u32[]{:S(2)}) collective-permute-start(bf16[128,8192]{1,0:T(8,128)(2,1)S(1)} %get-tuple-element.24), channel_id=1, source_target_pairs={{0,24},{8,0},{16,8},{24,16},{1,25},{9,1},{17,9},{25,17},{2,26},{10... | collective-permute-start | bytes 6291464 | tf_op jit(solution)/shard_map/ppermute | solution.py:114
  284.1 25.8 %collective-permute-start.2 = (bf16[128,8192]{1,0:T(8,128)(2,1)}, bf16[128,8192]{1,0:T(8,128)(2,1)}, u32[]{:S(2)}, u32[]{:S(2)}) collective-permute-start(bf16[128,8192]{1,0:T(8,128)(2,1)} %collective-permute-done), channel_id=1, source_target_pairs={{0,8},{8,16},{16,24},{24,0},{1,9},{9,17},{17,25},{25,1},{2,10},{10... | collective-permute-start | bytes 6291464 | tf_op jit(solution)/shard_map/ppermute | solution.py:109
Sparse Core Ops, SparseCore 0:
  11.9 64.9 all-gather.1
  329.0 66.1 reduce-scatter.4
Sparse Core Ops, SparseCore 1:
  46.3 128.4 reduce-scatter.2
